TPU v7x, 128 devices: a whole 4x4x4 slice. The times are simulated.
128 devices in a mesh: row: 8 (over z, core), col: 16 (over x, y).
Axes of the slice: x: 4, y: 4, z: 4, core: 2. Of those that a mesh axis runs over, the one named last changes fastest.
Arguments:
- edge_code: int32 [128, 4096], P(('row', 'col')), may hold values from 0 to 1572863
- edge_weight: bfloat16 [128, 4096], P(('row', 'col')), may hold values from 1 to 64
- edge_count: int32 [128, 128], P(('row', 'col')), may hold values from 0 to 32, as said below
- tile_blocks: int32 [128, 4, 2], P(('row', 'col')), may hold values from 0 to 127
- hub_blocks: int32 [8, 2, 2], P('row'), may hold values from 0 to 127
- node_degree: float32 [128, 512], P(('row', 'col')), may hold values from 1 to 16
Outputs:
- owned_tiles: float32 [512, 512, 512], P(('row', 'col'))
- hub_tiles: float32 [8192, 512], P(('row', 'col'))
Inputs may be any that keep to these rules, and one draw needn't show every extreme that they name: `edge_count`: at most 32 used slots from one device to another; in every draw some device receives 32 used slots from every device, and the loads of destinations differ widely.
All inputs are finite; a program needn't handle non-finite values.
Results may differ from a plain program's by a relative error of at most 0.0003.
Values may be sent and summed in bfloat16 or wider, within the bound.
A program may use at most 64 MiB of HBM per device.

v0:
```python
import jax
import jax.numpy as jnp
from jax import lax
from jax.sharding import Mesh
from jax.sharding import PartitionSpec as P

TILE = 512
TILES_DEV = 4
HUBS = 2
CAP = 32
ROW = ("row_0", "row_1")
COL = ("col_0", "col_1")
ROW_COL = ("row_0", "row_1", "col_0", "col_1")


def cut_along(x, dim, size):
    before, after = (x.shape[:dim], x.shape[dim + 1 :])
    return jnp.moveaxis(x.reshape(*before, size, -1, *after), dim, 0)


def in_order(blocks, dim):
    blocks = jnp.moveaxis(blocks, 0, dim)
    dims = blocks.shape
    return blocks.reshape(*dims[:dim], dims[dim] * dims[dim + 1], *dims[dim + 2 :])


def one_exchange(x, axis, axes, splits, concats):
    sizes = [lax.axis_size(a) for a in axes]
    blocks = cut_along(x, splits[0], sizes[0])
    blocks = jnp.moveaxis(cut_along(blocks, splits[1] + 1, sizes[1]), 0, 1)
    inside = blocks.shape[2:]
    blocks = blocks.reshape(-1, *inside)
    blocks = lax.all_to_all(blocks, axis, split_axis=0, concat_axis=0, tiled=True)
    blocks = in_order(blocks.reshape(*sizes, *inside), concats[0] + 1)
    return in_order(blocks, concats[1])


def stacked_from(x, axes, order):
    blocks = x[None]
    for k in order:
        blocks = lax.all_gather(blocks, axes[k], axis=0, tiled=True)
    block = [lax.axis_size(axes[k]) for k in reversed(order)]
    blocks = blocks.reshape(*block, *x.shape)
    turned = sorted(range(len(order)), key=lambda place: order[len(order) - 1 - place])
    return blocks.transpose(*turned, *range(len(order), blocks.ndim)).reshape(-1, *x.shape)


def gather_axes(x, axes, order, dim):
    return in_order(stacked_from(x, axes, order), dim)


def sum_at_owner(x, axis, dim):
    size = lax.axis_size(axis)
    blocks = lax.all_to_all(cut_along(x, dim, size), axis, 0, 0, tiled=True)
    return jnp.sum(blocks.astype(jnp.float32), axis=0)


def lookup(indices, degrees):
    selector = (indices[:, None] == jnp.arange(degrees.shape[0], dtype=jnp.int32)[None, :]).astype(
        jnp.float32
    )
    return jnp.dot(selector, degrees, precision=lax.Precision.HIGHEST)


def accumulate_rows(edge_codes, weights, row_count):
    total_edges = edge_codes.shape[0]
    block = 512
    row_keys = jnp.arange(row_count, dtype=jnp.int32)
    col_keys = jnp.arange(TILE, dtype=jnp.int32)

    def step_block(turn, totals):
        start = turn * block
        part_codes = lax.dynamic_slice_in_dim(edge_codes, start, block)
        part_weights = lax.dynamic_slice_in_dim(weights, start, block)
        left_side = jnp.where(
            part_codes[:, None] // TILE == row_keys[None, :],
            part_weights[:, None],
            jnp.zeros((), jnp.bfloat16),
        )
        right_side = (part_codes[:, None] % TILE == col_keys[None, :]).astype(jnp.bfloat16)
        return totals + lax.dot_general(
            left_side, right_side, (((0,), (0,)), ((), ())), preferred_element_type=jnp.float32
        )

    return lax.fori_loop(
        0, total_edges // block, step_block, jnp.zeros((row_count, TILE), jnp.float32)
    )


def shards(edge_code, edge_weight, edge_count, tile_blocks, hub_blocks, node_degree):
    n_row = lax.axis_size(ROW)
    n_col = lax.axis_size(COL)
    devices = n_row * n_col
    edge_codes, weights, counts = (
        one_exchange(edge_code.reshape(n_row, n_col, CAP), ROW_COL, (ROW, COL), (0, 1), (0, 1)),
        one_exchange(edge_weight.reshape(n_row, n_col, CAP), ROW_COL, (ROW, COL), (0, 1), (0, 1)),
        one_exchange(edge_count.reshape(n_row, n_col, 1), ROW_COL, (ROW, COL), (0, 1), (0, 1)),
    )
    edge_codes = edge_codes.reshape(devices, CAP)
    weights = weights.reshape(devices, CAP)
    counts = counts.reshape(devices, 1)
    usable = jnp.arange(CAP, dtype=jnp.int32)[None, :] < counts
    weights = jnp.where(usable, weights, jnp.zeros((), jnp.bfloat16)).reshape(-1)
    edge_codes = edge_codes.reshape(-1)
    degrees = gather_axes(node_degree, ROW_COL, (0, 2, 3, 1), 0)
    scaling = jnp.sum(degrees) / degrees.size
    slab_rows = HUBS * TILE // n_col
    offset = lax.axis_index(COL) * slab_rows
    totals = accumulate_rows(edge_codes, weights, (TILES_DEV + HUBS) * TILE)
    owned = totals[: TILES_DEV * TILE].reshape(TILES_DEV, TILE, TILE)
    summed = sum_at_owner(totals[TILES_DEV * TILE :].astype(jnp.bfloat16), COL, 0)
    blocks = tile_blocks[0]
    row_degree = lookup(blocks[:, 0], degrees)
    col_degree = lookup(blocks[:, 1], degrees)
    owned_tiles = jnp.log(
        jnp.maximum(scaling * owned / (row_degree[:, :, None] * col_degree[:, None, :]), 1.0)
    )
    hub_rows = lookup(hub_blocks[0][:, 0], degrees).reshape(-1)
    hub_row_degree = lax.dynamic_slice_in_dim(hub_rows, offset, slab_rows)
    hub_cols = lookup(hub_blocks[0][:, 1], degrees)
    hub_index = (offset + jnp.arange(slab_rows, dtype=jnp.int32)) // TILE
    selector = (hub_index[:, None] == jnp.arange(HUBS, dtype=jnp.int32)[None, :]).astype(
        jnp.float32
    )
    hub_col_degree = jnp.dot(selector, hub_cols, precision=lax.Precision.HIGHEST)
    hub_tiles = jnp.log(
        jnp.maximum(scaling * summed / (hub_row_degree[:, None] * hub_col_degree), 1.0)
    )
    return (owned_tiles, hub_tiles)


def solution(mesh):
    split = Mesh(mesh.devices.reshape(4, 2, 4, 4), ("row_0", "row_1", "col_0", "col_1"))
    placed = (
        P(ROW_COL, None),
        P(ROW_COL, None),
        P(ROW_COL, None),
        P(ROW_COL, None, None),
        P(ROW, None, None),
        P(ROW_COL, None),
    )
    return jax.shard_map(
        shards,
        mesh=split,
        in_specs=placed,
        out_specs=(P(ROW_COL, None, None), P(ROW_COL, None)),
        check_vma=False,
    )
```

profile of v0, /device:TPU:0, one launch (start us, length us, event | category | flops | bytes accessed | tf_op | source)
XLA Modules:
  0.0 174.7 jit_solution(8583765645140113446)
XLA Ops:
  0.6 1.4 copy.16
  2.0 11.2 %all-to-all-start.1 = ((s32[128,1,1,1]{3,2,1,0:T(1,128)}), s32[128,1,1,1]{3,2,1,0:T(1,128)S(1)}, u32[]{:S(2)}, u32[]{:S(2)}) async-start(s32[128,1,1,1]{3,2,1,0:T(1,128)} %copy.16), calls=%async_computation.1 | async-start | bytes 131072 | tf_op jit(solution)/shard_map/all_to_all | solution.py:33
  13.2 0.8 slice_bitcast_fusion.1
  14.0 1.0 slice_reduce_fusion.1
  15.0 11.1 %all-gather.4 = f32[4,1,512]{2,1,0:T(1,128)S(1)} all-gather(f32[1,1,512]{2,1,0:T(1,128)} %bitcast.64), channel_id=2, replica_groups=mesh['row_0'=4,'row_1'=2,'col_0'=4,'col_1'=4] {'row_0'}, dimensions={0}, use_global_device_ids=true | all-gather | bytes 10240 | tf_op jit(solution)/shard_map/all_gather | solution.py:41
  26.1 12.2 %all-gather.5 = f32[4,4,512]{2,1,0:T(4,128)S(1)} all-gather(f32[1,4,512]{2,1,0:T(4,128)S(1)} %copy.14), channel_id=3, replica_groups=mesh['row_0'=4,'row_1'=2,'col_0'=4,'col_1'=4] {'col_0'}, dimensions={0}, use_global_device_ids=true | all-gather | bytes 40960 | tf_op jit(solution)/shard_map/all_gather | solution.py:41
  38.3 0.5 broadcast.148
  38.9 1.4 reduce.13
  40.3 0.7 reshape_transpose_transpose_reshape_reshape_reshape.9
  41.0 12.4 %all-gather.2 = f32[64,512]{1,0:T(8,128)S(1)} all-gather(f32[16,512]{1,0:T(8,128)S(1)} %reshape.108), channel_id=4, replica_groups=mesh['row_0'=4,'row_1'=2,'col_0'=4,'col_1'=4] {'col_1'}, dimensions={0}, use_global_device_ids=true | all-gather | bytes 163840 | tf_op jit(solution)/shard_map/all_gather | solution.py:41
  53.4 2.0 %all-gather.3 = f32[128,512]{1,0:T(8,128)S(1)} all-gather(f32[64,512]{1,0:T(8,128)S(1)} %all-gather.2), channel_id=5, replica_groups=mesh['row_0'=4,'row_1'=2,'col_0'=4,'col_1'=4] {'row_1'}, dimensions={0}, use_global_device_ids=true | all-gather | bytes 393216 | tf_op jit(solution)/shard_map/all_gather | solution.py:41
  55.4 0.2 copy.22
  55.6 0.1 reshape_reshape.8
  55.7 0.2 fusion.18
  55.9 0.2 convolution_bitcast_fusion
  56.1 0.2 fusion.17
  56.4 0.2 fusion.16
  56.6 0.8 reduce.6
  57.4 0.7 reshape_transpose_transpose_reshape_reshape_reshape.12
  58.1 0.7 reduce_sum.18
  59.6 7.7 %all-to-all-start.2 = ((bf16[128,1,1,32]{3,2,1,0:T(2,128)(2,1)}), bf16[128,1,1,32]{3,2,1,0:T(2,128)(2,1)S(1)}, u32[]{:S(2)}, u32[]{:S(2)}) async-start(bf16[128,1,1,32]{3,2,1,0:T(2,128)(2,1)} %reshape_transpose_transpose_reshape_reshape_reshape.12), calls=%async_computation.2 | async-start | bytes 131072 | tf_op jit(solution)/shard_map/all_to_all | solution.py:33
  67.3 2.4 %reduce.5 = s32[128]{0:T(128)S(1)} reduce(s32[128,1,1,1]{3,2,1,0:T(1,128)S(1)} %all-to-all-done.1, s32[]{:T(128)} %constant.122.clone.1), dimensions={1,2,3}, to_apply=%all_to_all.13.reduce_sub_computation | reduce | bytes 1028 | tf_op jit(solution)/shard_map/all_to_all | solution.py:33
  69.8 0.1 lt.51
  69.8 0.1 iota_compare_fusion.3
  69.9 0.1 lt.54
  70.0 6.8 %all-to-all-done.2 = bf16[128,1,1,32]{3,2,1,0:T(2,128)(2,1)S(1)} async-done(((bf16[128,1,1,32]{3,2,1,0:T(2,128)(2,1)}), bf16[128,1,1,32]{3,2,1,0:T(2,128)(2,1)S(1)}, u32[]{:S(2)}, u32[]{:S(2)}) %all-to-all-start.2) | async-done | bytes 8224 | tf_op jit(solution)/shard_map/all_to_all | solution.py:33
  76.8 4.6 %all-to-all-start = ((s32[128,1,1,32]{3,2,1,0:T(1,128)}), s32[128,1,1,32]{3,2,1,0:T(1,128)S(1)}, u32[]{:S(2)}, u32[]{:S(2)}) async-start(s32[128,1,1,32]{3,2,1,0:T(1,128)} %bitcast.2), calls=%async_computation | async-start | bytes 131072 | tf_op jit(solution)/shard_map/all_to_all | solution.py:33
  81.4 0.1 reshape_reshape.7
  81.5 9.3 %all-to-all-done = s32[128,1,1,32]{3,2,1,0:T(1,128)S(1)} async-done(((s32[128,1,1,32]{3,2,1,0:T(1,128)}), s32[128,1,1,32]{3,2,1,0:T(1,128)S(1)}, u32[]{:S(2)}, u32[]{:S(2)}) %all-to-all-start) | async-done | bytes 16416 | tf_op jit(solution)/shard_map/all_to_all | solution.py:33
  90.9 58.6 %while.16 = (s32[]{:T(128)}, f32[3072,512]{1,0:T(8,128)}, s32[4096]{0:T(1024)S(1)}, bf16[4096]{0:T(1024)(128)(2,1)S(1)}, s32[]{:T(128)}, /*index=5*/s32[]{:T(128)}, s32[]{:T(128)}, s32[]{:T(128)}) while((s32[]{:T(128)}, f32[3072,512]{1,0:T(8,128)}, s32[4096]{0:T(1024)S(1)}, bf16[4096]{0:T(1024)(128)(2,1)S(1)}, s32[]{:T(128)}, ...), condition=%wide.region_2.3_spmd.clone, body=%wide.region_1.2_spmd.clone.sunk | while | flops 1617176064 | bytes 12596381 | solution.py:85
  91.0 0.1 add_select_fusion.3
  91.1 4.7 %select_add_fusion.2 = f32[3072,512]{1,0:T(8,128)} fusion(f32[3072,512]{1,0:T(8,128)} %get-tuple-element.231, s32[512]{0:T(512)S(1)} %get-tuple-element.220, pred[]{:T(512)S(6)} %compare.23, bf16[512]{0:T(512)(128)(2,1)S(1)} %dynamic_slice.35, s32[512]{0:T(512)S(1)} %get-tuple-element.221), kind=kOutput, calls=%fused_computation.3.clone.1 | convolution fusion | flops 1617166336 | bytes 12588033 | tf_op jit(solution)/shard_map/while/body/eval_jaxpr/dot_general | solution.py:81
  95.9 0.1 add_select_fusion.3
  96.0 7.5 %select_add_fusion.2 = f32[3072,512]{1,0:T(8,128)} fusion(f32[3072,512]{1,0:T(8,128)} %get-tuple-element.231, s32[512]{0:T(512)S(1)} %get-tuple-element.220, pred[]{:T(512)S(6)} %compare.23, bf16[512]{0:T(512)(128)(2,1)S(1)} %dynamic_slice.35, s32[512]{0:T(512)S(1)} %get-tuple-element.221), kind=kOutput, calls=%fused_computation.3.clone.1 | convolution fusion | flops 1617166336 | bytes 12588033 | tf_op jit(solution)/shard_map/while/body/eval_jaxpr/dot_general | solution.py:81
  103.6 0.1 add_select_fusion.3
  103.7 7.5 %select_add_fusion.2 = f32[3072,512]{1,0:T(8,128)} fusion(f32[3072,512]{1,0:T(8,128)} %get-tuple-element.231, s32[512]{0:T(512)S(1)} %get-tuple-element.220, pred[]{:T(512)S(6)} %compare.23, bf16[512]{0:T(512)(128)(2,1)S(1)} %dynamic_slice.35, s32[512]{0:T(512)S(1)} %get-tuple-element.221), kind=kOutput, calls=%fused_computation.3.clone.1 | convolution fusion | flops 1617166336 | bytes 12588033 | tf_op jit(solution)/shard_map/while/body/eval_jaxpr/dot_general | solution.py:81
  111.4 7.5 %select_add_fusion.2 = f32[3072,512]{1,0:T(8,128)} fusion(f32[3072,512]{1,0:T(8,128)} %get-tuple-element.231, s32[512]{0:T(512)S(1)} %get-tuple-element.220, pred[]{:T(512)S(6)} %compare.23, bf16[512]{0:T(512)(128)(2,1)S(1)} %dynamic_slice.35, s32[512]{0:T(512)S(1)} %get-tuple-element.221), kind=kOutput, calls=%fused_computation.3.clone.1 | convolution fusion | flops 1617166336 | bytes 12588033 | tf_op jit(solution)/shard_map/while/body/eval_jaxpr/dot_general | solution.py:81
  119.0 7.5 %select_add_fusion.2 = f32[3072,512]{1,0:T(8,128)} fusion(f32[3072,512]{1,0:T(8,128)} %get-tuple-element.231, s32[512]{0:T(512)S(1)} %get-tuple-element.220, pred[]{:T(512)S(6)} %compare.23, bf16[512]{0:T(512)(128)(2,1)S(1)} %dynamic_slice.35, s32[512]{0:T(512)S(1)} %get-tuple-element.221), kind=kOutput, calls=%fused_computation.3.clone.1 | convolution fusion | flops 1617166336 | bytes 12588033 | tf_op jit(solution)/shard_map/while/body/eval_jaxpr/dot_general | solution.py:81
  126.7 7.5 %select_add_fusion.2 = f32[3072,512]{1,0:T(8,128)} fusion(f32[3072,512]{1,0:T(8,128)} %get-tuple-element.231, s32[512]{0:T(512)S(1)} %get-tuple-element.220, pred[]{:T(512)S(6)} %compare.23, bf16[512]{0:T(512)(128)(2,1)S(1)} %dynamic_slice.35, s32[512]{0:T(512)S(1)} %get-tuple-element.221), kind=kOutput, calls=%fused_computation.3.clone.1 | convolution fusion | flops 1617166336 | bytes 12588033 | tf_op jit(solution)/shard_map/while/body/eval_jaxpr/dot_general | solution.py:81
  134.4 7.5 %select_add_fusion.2 = f32[3072,512]{1,0:T(8,128)} fusion(f32[3072,512]{1,0:T(8,128)} %get-tuple-element.231, s32[512]{0:T(512)S(1)} %get-tuple-element.220, pred[]{:T(512)S(6)} %compare.23, bf16[512]{0:T(512)(128)(2,1)S(1)} %dynamic_slice.35, s32[512]{0:T(512)S(1)} %get-tuple-element.221), kind=kOutput, calls=%fused_computation.3.clone.1 | convolution fusion | flops 1617166336 | bytes 12588033 | tf_op jit(solution)/shard_map/while/body/eval_jaxpr/dot_general | solution.py:81
  142.1 7.5 %select_add_fusion.2 = f32[3072,512]{1,0:T(8,128)} fusion(f32[3072,512]{1,0:T(8,128)} %get-tuple-element.231, s32[512]{0:T(512)S(1)} %get-tuple-element.220, pred[]{:T(512)S(6)} %compare.23, bf16[512]{0:T(512)(128)(2,1)S(1)} %dynamic_slice.35, s32[512]{0:T(512)S(1)} %get-tuple-element.221), kind=kOutput, calls=%fused_computation.3.clone.1 | convolution fusion | flops 1617166336 | bytes 12588033 | tf_op jit(solution)/shard_map/while/body/eval_jaxpr/dot_general | solution.py:81
  149.6 2.7 %slice.32 = bf16[1024,512]{1,0:T(8,128)(2,1)} slice(f32[3072,512]{1,0:T(8,128)} %get-tuple-element.159), slice={[2048:3072], [0:512]} | slice | bytes 2097152 | tf_op jit(solution)/shard_map/slice | solution.py:111
  152.3 3.7 %all-to-all-start.3 = ((bf16[16,64,512]{2,1,0:T(8,128)(2,1)}), bf16[16,64,512]{2,1,0:T(8,128)(2,1)S(1)}, u32[]{:S(2)}, u32[]{:S(2)}) async-start(bf16[16,64,512]{2,1,0:T(8,128)(2,1)} %bitcast.19), calls=%async_computation.3 | async-start | bytes 2097152 | tf_op jit(solution)/shard_map/all_to_all | solution.py:54
  156.0 2.7 %slice_multiply_fusion = f32[2048,512]{1,0:T(8,128)S(1)} fusion(f32[3072,512]{1,0:T(8,128)} %get-tuple-element.159, f32[]{:T(128)S(6)} %div.35), kind=kLoop, calls=%fused_computation.20 | loop fusion | flops 1048576 | bytes 8388612 | tf_op jit(solution)/shard_map/mul | solution.py:116
  158.7 2.7 %maximum_log_fusion = f32[4,512,512]{2,1,0:T(8,128)} fusion(f32[4,512,512]{2,1,0:T(8,128)S(1)} %bitcast.56, f32[4,512]{1,0:T(4,128)S(1)} %fusion.17, f32[4,512]{1,0:T(4,128)S(1)} %fusion.16), kind=kLoop, calls=%fused_computation.19 | loop fusion | flops 3145728 | bytes 8404992 | tf_op jit(solution)/shard_map/log | solution.py:115
  161.3 12.3 %all-to-all-done.3 = bf16[16,64,512]{2,1,0:T(8,128)(2,1)S(1)} async-done(((bf16[16,64,512]{2,1,0:T(8,128)(2,1)}), bf16[16,64,512]{2,1,0:T(8,128)(2,1)S(1)}, u32[]{:S(2)}, u32[]{:S(2)}) %all-to-all-start.3) | async-done | bytes 1048608 | tf_op jit(solution)/shard_map/all_to_all | solution.py:54
  173.7 0.1 convert_reduce_fusion
  173.8 0.9 fusion.14
  (25 shorter events, 1.4 us)
Async XLA Ops:
  2.0 57.6 %all-to-all-start.1 = ((s32[128,1,1,1]{3,2,1,0:T(1,128)}), s32[128,1,1,1]{3,2,1,0:T(1,128)S(1)}, u32[]{:S(2)}, u32[]{:S(2)}) async-start(s32[128,1,1,1]{3,2,1,0:T(1,128)} %copy.16), calls=%async_computation.1 | async-start | bytes 131072 | tf_op jit(solution)/shard_map/all_to_all | solution.py:33
  59.6 17.2 %all-to-all-start.2 = ((bf16[128,1,1,32]{3,2,1,0:T(2,128)(2,1)}), bf16[128,1,1,32]{3,2,1,0:T(2,128)(2,1)S(1)}, u32[]{:S(2)}, u32[]{:S(2)}) async-start(bf16[128,1,1,32]{3,2,1,0:T(2,128)(2,1)} %reshape_transpose_transpose_reshape_reshape_reshape.12), calls=%async_computation.2 | async-start | bytes 131072 | tf_op jit(solution)/shard_map/all_to_all | solution.py:33
  76.8 14.0 %all-to-all-start = ((s32[128,1,1,32]{3,2,1,0:T(1,128)}), s32[128,1,1,32]{3,2,1,0:T(1,128)S(1)}, u32[]{:S(2)}, u32[]{:S(2)}) async-start(s32[128,1,1,32]{3,2,1,0:T(1,128)} %bitcast.2), calls=%async_computation | async-start | bytes 131072 | tf_op jit(solution)/shard_map/all_to_all | solution.py:33
  152.3 21.3 %all-to-all-start.3 = ((bf16[16,64,512]{2,1,0:T(8,128)(2,1)}), bf16[16,64,512]{2,1,0:T(8,128)(2,1)S(1)}, u32[]{:S(2)}, u32[]{:S(2)}) async-start(bf16[16,64,512]{2,1,0:T(8,128)(2,1)} %bitcast.19), calls=%async_computation.3 | async-start | bytes 2097152 | tf_op jit(solution)/shard_map/all_to_all | solution.py:54
where the time goes:
time: 176 us; the launch traced here: 175 us
  matrix products  59.2 us (34%)
  blocking collectives  37.8 us (21%)
  waiting for transfers between devices  28.4 us (16%)
  starting transfers between devices  27.1 us (15%)
  other arithmetic  11.5 us (7%)
  local copies, waits for them, and re-layouts  9.26 us (5%)
    dot_general x8, matrix products, step_block(): lax.dot_general(left_side, right_side, (((0,), (0,)), ((), ())), preferre...  57.3 us
    all_gather x4, blocking collectives, stacked_from(): blocks = lax.all_gather(blocks, axes[k], axis=0, tiled=True)  37.8 us
    all_to_all x3, starting transfers between devices, one_exchange(): lax.all_to_all(blocks, axis, split_axis=0, concat_axis=0, tiled=True)  23.5 us
    all_to_all x3, waiting for transfers between devices, one_exchange(): lax.all_to_all(blocks, axis, split_axis=0, concat_axis=0, tiled=True)  16.1 us
    all_to_all x1, waiting for transfers between devices, sum_at_owner(): blocks = lax.all_to_all(cut_along(x, dim, size), axis, 0, 0, tiled=True)  12.3 us
    all_to_all x1, starting transfers between devices, sum_at_owner(): blocks = lax.all_to_all(cut_along(x, dim, size), axis, 0, 0, tiled=True)  3.65 us
  transfers between devices with their start and end apart: 4, of which 3 were waited for; matrix products, arithmetic and copies ran while one was open for 9% of the time, Pallas kernels for 0%

commit v1 on v0

v1 whole, which is shorter than its diff:
```python
import jax
import jax.numpy as jnp
from jax import lax
from jax.experimental import pallas as pl
from jax.experimental.pallas import tpu as pltpu
from jax.sharding import PartitionSpec as P

TILE = 512
TILES_DEV = 4
HUBS = 2
CAP = 32
N_ROW = 8
N_COL = 16
LANES = 128
CHUNK = 256
CHUNKS = TILES_DEV * TILE // CHUNK
DEPTH = 8
MESH = pl.DeviceIdType.MESH
F32 = jnp.float32
BF16 = jnp.bfloat16
NT = (((1,), (1,)), ((), ()))


def iota(shape, dim):
    return lax.broadcasted_iota(jnp.int32, shape, dim)


def exchange_kernel(
    code_ref, weight_ref, count_ref, degree_ref, slots_ref, degrees_ref,
    message, wide, row_send, row_recv, col_send, col_recv, local_sem,
):
    row = lax.axis_index("row")
    col = lax.axis_index("col")
    row_peers = [lax.rem(row + k, N_ROW) for k in range(1, N_ROW)]
    col_peers = [lax.rem(col + k, N_COL) for k in range(1, N_COL)]

    barrier = pltpu.get_barrier_semaphore()
    for peer in row_peers:
        pl.semaphore_signal(barrier, inc=1, device_id=(peer, col), device_id_type=MESH)
    for peer in col_peers:
        pl.semaphore_signal(barrier, inc=1, device_id=(row, peer), device_id_type=MESH)

    device = iota((32, LANES), 1)
    place = iota((32, LANES), 0)
    counts = jnp.where(device // 4 == place, jnp.broadcast_to(count_ref[...], (32, LANES)), 0)
    spread = (iota((LANES, LANES), 0) % 4 == iota((LANES, LANES), 1) // CAP).astype(BF16)
    counts = jnp.dot(counts.astype(BF16), spread, preferred_element_type=F32)
    for g in range(32):
        wide[pl.ds(g, 1), :] = weight_ref[:, pl.ds(g * LANES, LANES)].astype(F32)
    weights = jnp.where((device % CAP).astype(F32) < counts, wide[...], 0.0)
    for r in range(N_ROW):
        message[r, pl.ds(4, 4), :] = weights[4 * r : 4 * r + 4]
        for g in range(4):
            lanes = pl.ds((4 * r + g) * LANES, LANES)
            message[r, pl.ds(g, 1), :] = code_ref[:, lanes].astype(F32)

    pl.semaphore_wait(barrier, N_ROW + N_COL - 2)

    started = []
    for peer in row_peers:
        for part, (src, dst) in enumerate((
            (message.at[peer], slots_ref.at[col, row]),
            (degree_ref, degrees_ref.at[col, row]),
        )):
            copy = pltpu.make_async_remote_copy(
                src_ref=src, dst_ref=dst, send_sem=row_send.at[part], recv_sem=row_recv.at[part],
                device_id=(peer, col), device_id_type=MESH,
            )
            copy.start()
    own = (
        pltpu.make_async_copy(message.at[row], slots_ref.at[col, row], local_sem.at[0]),
        pltpu.make_async_copy(degree_ref, degrees_ref.at[col, row], local_sem.at[1]),
    )
    for copy in own:
        copy.start()
    for copy in own:
        copy.wait()
    others = pl.ds(0, N_ROW - 1)
    whole = (slots_ref.at[0, others], degrees_ref.at[0, others])
    for part in range(2):
        pltpu.make_async_copy(whole[part], whole[part], row_recv.at[part]).wait()

    for peer in col_peers:
        for part, ref in enumerate((slots_ref, degrees_ref)):
            pltpu.make_async_remote_copy(
                src_ref=ref.at[col], dst_ref=ref.at[col],
                send_sem=col_send.at[part], recv_sem=col_recv.at[part],
                device_id=(row, peer), device_id_type=MESH,
            ).start()
    for part in range(2):
        pltpu.make_async_copy(whole[part], whole[part], row_send.at[part]).wait()
    others = pl.ds(0, N_COL - 1)
    whole = (slots_ref.at[others], degrees_ref.at[others])
    for part in range(2):
        pltpu.make_async_copy(whole[part], whole[part], col_recv.at[part]).wait()
        pltpu.make_async_copy(whole[part], whole[part], col_send.at[part]).wait()


def exchange(code, weight, count, degree):
    vmem = pl.BlockSpec(memory_space=pltpu.VMEM)
    return pl.pallas_call(
        exchange_kernel,
        out_shape=(
            jax.ShapeDtypeStruct((N_COL, N_ROW, 8, LANES), F32),
            jax.ShapeDtypeStruct((N_COL, N_ROW, 4, LANES), F32),
        ),
        in_specs=[vmem] * 4,
        out_specs=(vmem, vmem),
        scratch_shapes=[
            pltpu.VMEM((N_ROW, 8, LANES), F32),
            pltpu.VMEM((32, LANES), F32),
            pltpu.SemaphoreType.DMA((2,)),
            pltpu.SemaphoreType.DMA((2,)),
            pltpu.SemaphoreType.DMA((2,)),
            pltpu.SemaphoreType.DMA((2,)),
            pltpu.SemaphoreType.DMA((2,)),
        ],
        compiler_params=pltpu.CompilerParams(
            collective_id=0, has_side_effects=True, vmem_limit_bytes=16 << 20
        ),
    )(code, weight, count, degree)


def one_hot(keys, rows):
    wide = jnp.broadcast_to(keys.astype(BF16), (rows, keys.shape[1]))
    return wide == iota((rows, keys.shape[1]), 0).astype(BF16)


def weighted(mask, values):
    return jnp.where(mask, jnp.broadcast_to(values.astype(BF16), mask.shape), jnp.zeros((), BF16))


def ones_where(mask):
    return jnp.where(mask, jnp.ones((), BF16), jnp.zeros((), BF16))


def two_rows(x, index):
    return jnp.concatenate([x[2 * index : 2 * index + 1], x[2 * index + 1 : 2 * index + 2]], axis=1)


def stored(block):
    return lax.rem(block, N_COL) * N_ROW + block // N_COL


def tile_kernel(
    slots_ref, degrees_ref, blocks_ref, hubs_ref, owned_ref, hub_ref,
    keys, fields, total, hub_total, staged, gathered, out_sem,
):
    col = lax.axis_index("col")

    scaling = jnp.sum(jnp.sum(degrees_ref[...], axis=0)) / (N_ROW * N_COL * TILE)
    gathered[...] = jnp.ones_like(gathered)
    for t in range(TILES_DEV):
        gathered[pl.ds(4 * t, 4), :] = degrees_ref[stored(blocks_ref[0, t, 0])]
    hub = col // 8
    hub_row = degrees_ref[stored(hubs_ref[0, hub, 0]), pl.ds(lax.rem(col, 8) // 2, 1), :]
    gathered[pl.ds(16, 8), :] = pltpu.roll(
        jnp.broadcast_to(hub_row, (8, LANES)), 64 * lax.rem(col, 2), axis=1
    )
    turned = (scaling / gathered[...]).T

    upper = iota((8, LANES), 0) < 4
    slab = 32 + col

    def collect(i, carry):
        tops, hits = carry
        first = slots_ref[pl.ds(16 * i, 8), :]
        second = slots_ref[pl.ds(16 * i + 8, 8), :]
        code = jnp.where(upper, first, pltpu.roll(second, 4, axis=0)).astype(jnp.int32)
        weight = jnp.where(upper, pltpu.roll(first, 4, axis=0), second)
        hit = jnp.logical_and(code >> 15 == slab, weight > 0.0)
        key = jnp.where(hit, ((code & 32767) << 14) + (weight * 128.0).astype(jnp.int32), 0)
        keys[pl.ds(8 * i, 8), :] = key
        kept = []
        for top in tops:
            kept.append(jnp.maximum(top, key))
            key = jnp.minimum(top, key)
        return tuple(kept), hits + hit.astype(jnp.int32)

    none = jnp.zeros((8, LANES), jnp.int32)
    tops, hits = lax.fori_loop(0, 64, collect, ((none,) * DEPTH, none), unroll=4)
    for d in range(DEPTH):
        keys[pl.ds(512 + 8 * d, 8), :] = tops[d]
    deepest = jnp.max(hits)
    fits = deepest <= DEPTH
    first_group = jnp.where(fits, 64, 0)
    groups = jnp.where(fits, deepest, 64)

    hub_total[...] = jnp.zeros_like(hub_total)

    def add_hub(i, _):
        key = keys[pl.ds(8 * (first_group + i), 8), :]
        cell = key >> 14
        weight = (key & 16383).astype(F32) * (1.0 / 128.0)
        left = ((cell >> 8) & 1) * 64 + (cell >> 9)
        left, right = left.astype(F32), (cell & 255).astype(F32)
        part = jnp.zeros((LANES, 256), F32)
        for p in range(4):
            part += lax.dot_general(
                weighted(one_hot(two_rows(left, p), LANES), two_rows(weight, p)),
                ones_where(one_hot(two_rows(right, p), 256)),
                NT, preferred_element_type=F32,
            )
        hub_total[...] += part
        return 0

    lax.fori_loop(0, groups, add_hub, 0)
    hub_degree = 1.0 / degrees_ref[stored(hubs_ref[0, hub, 1])]
    for n in range(4):
        values = hub_total[pl.ds(64 * (n // 2), 64), pl.ds(LANES * (n % 2), LANES)]
        values = values * turned[0:64, 16:17] * hub_degree[n : n + 1]
        hub_ref[:, pl.ds(LANES * n, LANES)] = jnp.log(jnp.maximum(values, 1.0))

    lane = iota((32, LANES), 1)

    def own(line):
        block = slots_ref[pl.ds(line, LANES, stride=8), :]
        joined = jnp.zeros((32, LANES), F32)
        for g in range(4):
            shift = lax.rem(CAP * g - CAP * lax.rem(col, 4) + LANES, LANES)
            part = pltpu.roll(block[32 * g : 32 * g + 32], shift, axis=1)
            joined = jnp.where(lane // CAP == g, part, joined)
        return joined

    code = own(col // 4).astype(jnp.int32)
    weight = own(4 + col // 4)
    chunk = jnp.where(weight > 0.0, code >> 17, CHUNKS)

    member = [ones_where(chunk == q) for q in range(CHUNKS)]
    member = jnp.concatenate(member, axis=0)
    upto = ones_where(iota((LANES, LANES), 0) <= iota((LANES, LANES), 1))
    inside = jnp.dot(member, upto, preferred_element_type=F32)
    lines = jnp.dot(member, jnp.ones((LANES, LANES), BF16), preferred_element_type=F32)
    before = ones_where(iota((256, 256), 1) < iota((256, 256), 0))
    base = jnp.dot(before, lines.astype(BF16), preferred_element_type=F32)
    rank = base + inside - 1.0
    place = jnp.full((32, LANES), -1.0, F32)
    for q in range(CHUNKS):
        place = jnp.where(chunk == q, rank[32 * q : 32 * q + 32], place)
    place = place.astype(jnp.int32)
    starts = [jnp.max(base[32 * q : 32 * q + 1]).astype(jnp.int32) for q in range(CHUNKS)]
    starts.append(jnp.max(base[255:256] + lines[255:256]).astype(jnp.int32))

    high, low = (place >> 7).astype(F32), (place & 127).astype(F32)
    parts = (
        (code & 255).astype(F32),
        (((code >> 8) & 1) + 2 * (code >> 17)).astype(F32),
        ((code >> 9) & 255).astype(F32),
        weight,
    )
    moved = jnp.zeros((LANES, LANES), F32)
    for p in range(16):
        mask = one_hot(two_rows(high, p), 32)
        left = jnp.concatenate([weighted(mask, two_rows(part, p)) for part in parts], axis=0)
        right = ones_where(one_hot(two_rows(low, p), LANES))
        moved += lax.dot_general(left, right, NT, preferred_element_type=F32)
    flags = moved[32:64].astype(jnp.int32)
    column = moved[0:32] + ((flags & 1) * 256).astype(F32)
    fields[0] = moved[64:96] + ((flags >> 1) * 256).astype(F32)
    fields[1] = column
    fields[2] = column - 256.0
    fields[3] = moved[96:128]

    def out_copy(q):
        return pltpu.make_async_copy(
            staged.at[q % 2], owned_ref.at[q // 2, pl.ds(CHUNK * (q % 2), CHUNK)], out_sem.at[q % 2]
        )

    for q in range(CHUNKS):
        total[...] = jnp.zeros_like(total)

        def add_block(b, _, q=q):
            def line(f):
                return jnp.concatenate(
                    [fields[f, pl.ds(2 * b, 1), :], fields[f, pl.ds(2 * b + 1, 1), :]], axis=1
                )

            left = weighted(one_hot(line(0) - 256.0 * q, CHUNK), line(3))
            right = jnp.concatenate(
                [ones_where(one_hot(line(1), 256)), ones_where(one_hot(line(2), 256))], axis=0
            )
            total[...] += lax.dot_general(left, right, NT, preferred_element_type=F32)
            return 0

        last = jnp.where(starts[q + 1] > starts[q], (starts[q + 1] + 255) >> 8, starts[q] >> 8)
        lax.fori_loop(starts[q] >> 8, last, add_block, 0)
        if q >= 2:
            out_copy(q - 2).wait()
        tile = q // 2
        degree = 1.0 / degrees_ref[stored(blocks_ref[0, tile, 1])]
        for j in range(2):
            rows = turned[:, 4 * tile + 2 * (q % 2) + j][:, None]
            for n in range(4):
                values = total[pl.ds(LANES * j, LANES), pl.ds(LANES * n, LANES)]
                values = values * rows * degree[n : n + 1]
                staged[q % 2, pl.ds(LANES * j, LANES), pl.ds(LANES * n, LANES)] = jnp.log(
                    jnp.maximum(values, 1.0)
                )
        out_copy(q).start()
    out_copy(CHUNKS - 2).wait()
    out_copy(CHUNKS - 1).wait()


def tiles(slots, degrees, blocks, hubs):
    vmem = pl.BlockSpec(memory_space=pltpu.VMEM)
    smem = pl.BlockSpec(memory_space=pltpu.SMEM)
    return pl.pallas_call(
        tile_kernel,
        out_shape=(
            jax.ShapeDtypeStruct((TILES_DEV, TILE, TILE), F32),
            jax.ShapeDtypeStruct((HUBS * TILE // N_COL, TILE), F32),
        ),
        in_specs=[vmem, vmem, smem, smem],
        out_specs=(pl.BlockSpec(memory_space=pl.ANY), vmem),
        scratch_shapes=[
            pltpu.VMEM((576, LANES), jnp.int32),
            pltpu.VMEM((4, 32, LANES), F32),
            pltpu.VMEM((CHUNK, TILE), F32),
            pltpu.VMEM((LANES, 256), F32),
            pltpu.VMEM((2, CHUNK, TILE), F32),
            pltpu.VMEM((LANES, LANES), F32),
            pltpu.SemaphoreType.DMA((2,)),
        ],
        compiler_params=pltpu.CompilerParams(vmem_limit_bytes=32 << 20),
    )(slots, degrees, blocks, hubs)


def shards(edge_code, edge_weight, edge_count, tile_blocks, hub_blocks, node_degree):
    slots, degrees = exchange(edge_code, edge_weight, edge_count, node_degree.reshape(4, LANES))
    degrees = degrees.reshape(N_COL * N_ROW, 4, LANES)
    return tiles(slots.reshape(-1, LANES), degrees, tile_blocks, hub_blocks)


def solution(mesh):
    both = ("row", "col")
    return jax.shard_map(
        shards,
        mesh=mesh,
        in_specs=(
            P(both, None), P(both, None), P(both, None),
            P(both, None, None), P("row", None, None), P(both, None),
        ),
        out_specs=(P(both, None, None), P(both, None)),
        check_vma=False,
    )
```

time: 176 us -> 39.1 us (0.22)
  the two profiles are of different devices: /device:TPU:0 before, /device:TPU:24 now
where the time goes in v1:
time: 39.1 us
  Pallas kernels  34.2 us (87%)
  local copies, waits for them, and re-layouts  4.21 us (11%)
  between operations  0.65 us (2%)
    pallas_call x1, Pallas kernels, exchange(): pl.pallas_call(exchange_kernel, out_shape=(jax.ShapeDtypeStruct((N_COL, N...  23.8 us
    pallas_call x1, Pallas kernels, tiles(): pl.pallas_call(tile_kernel, out_shape=(jax.ShapeDtypeStruct((TILES_DEV, T...  10.4 us
    unnamed x11, local copies, waits for them, and re-layouts  4.21 us

profile of v1, /device:TPU:24, one launch (start us, length us, event | category | flops | bytes accessed | tf_op | source)
XLA Modules:
  0.0 39.1 jit_solution(18369217797367466343)
XLA Ops:
  0.6 0.8 %copy.8.blocks_ref = s32[1,4,2]{2,1,0:T(4,128)S(1)} copy(s32[1,4,2]{1,2,0:T(2,128)} %param.9) | data formatting | bytes 64 | tf_op args[3]
  1.4 0.0 copy-start
  1.4 0.7 %copy-done = s32[1,4096]{1,0:T(1,128)S(1)} copy-done((s32[1,4096]{1,0:T(1,128)S(1)}, s32[1,4096]{1,0:T(1,128)}, u32[]{:S(2)}) %copy-start) | copy-done | bytes 16408
  2.1 0.0 copy-start.1
  2.1 0.7 %copy-done.1 = bf16[1,4096]{1,0:T(2,128)(2,1)S(1)} copy-done((bf16[1,4096]{1,0:T(2,128)(2,1)S(1)}, bf16[1,4096]{1,0:T(2,128)(2,1)}, u32[]{:S(2)}) %copy-start.1) | copy-done | bytes 8216
  2.8 0.0 copy-start.2
  2.8 0.7 %copy-done.2 = f32[1,512]{1,0:T(1,128)S(1)} copy-done((f32[1,512]{1,0:T(1,128)S(1)}, f32[1,512]{1,0:T(1,128)}, u32[]{:S(2)}) %copy-start.2) | copy-done | bytes 2072
  3.5 0.0 copy-start.4
  3.5 0.7 %copy-done.4 = s32[1,128]{1,0:T(1,128)S(1)} copy-done((s32[1,128]{1,0:T(1,128)S(1)}, s32[1,128]{1,0:T(1,128)}, u32[]{:S(2)}) %copy-start.4) | copy-done | bytes 536
  4.2 23.8 %shard_map.77 = (f32[16,8,8,128]{3,2,1,0:T(8,128)S(1)}, f32[16,8,4,128]{3,2,1,0:T(4,128)S(1)}) custom-call(s32[1,4096]{1,0:T(1,128)S(1)} %copy-done, bf16[1,4096]{1,0:T(2,128)(2,1)S(1)} %copy-done.1, s32[1,128]{1,0:T(1,128)S(1)} %copy-done.4, f32[4,128]{1,0:T(4,128)S(1)} %bitcast.5), custom_call_target="tpu_custom_call" | custom-call | tf_op jit(solution)/shard_map/pallas_call | solution.py:101
  28.0 0.0 copy-start.3
  28.0 0.7 %copy-done.3 = s32[1,2,2]{2,1,0:T(2,128)S(1)} copy-done((s32[1,2,2]{2,1,0:T(2,128)S(1)}, s32[1,2,2]{2,1,0:T(2,128)}, u32[]{:S(2)}) %copy-start.3) | copy-done | bytes 40
  28.7 10.4 %shard_map.78 = (f32[4,512,512]{2,1,0:T(8,128)}, f32[64,512]{1,0:T(8,128)}) custom-call(f32[1024,128]{1,0:T(8,128)S(1)} %bitcast.3, f32[128,4,128]{2,1,0:T(4,128)S(1)} %bitcast.4, s32[1,4,2]{2,1,0:T(4,128)S(1)} %copy.8.blocks_ref, s32[1,2,2]{2,1,0:T(2,128)S(1)} %copy-done.3), custom_call_target="tpu_custom_call" | custom-call | tf_op jit(solution)/shard_map/pallas_call | solution.py:307
Async XLA Ops:
  1.4 0.7 %copy-start = (s32[1,4096]{1,0:T(1,128)S(1)}, s32[1,4096]{1,0:T(1,128)}, u32[]{:S(2)}) copy-start(s32[1,4096]{1,0:T(1,128)} %code_ref.1) | copy-start | bytes 49156
  2.1 0.7 %copy-start.1 = (bf16[1,4096]{1,0:T(2,128)(2,1)S(1)}, bf16[1,4096]{1,0:T(2,128)(2,1)}, u32[]{:S(2)}) copy-start(bf16[1,4096]{1,0:T(2,128)(2,1)} %weight_ref.1) | copy-start | bytes 24580
  2.8 0.7 %copy-start.2 = (f32[1,512]{1,0:T(1,128)S(1)}, f32[1,512]{1,0:T(1,128)}, u32[]{:S(2)}) copy-start(f32[1,512]{1,0:T(1,128)} %param.11) | copy-start | bytes 6148
  3.5 0.7 %copy-start.4 = (s32[1,128]{1,0:T(1,128)S(1)}, s32[1,128]{1,0:T(1,128)}, u32[]{:S(2)}) copy-start(s32[1,128]{1,0:T(1,128)} %count_ref.1) | copy-start | bytes 1540
  28.0 0.7 %copy-start.3 = (s32[1,2,2]{2,1,0:T(2,128)S(1)}, s32[1,2,2]{2,1,0:T(2,128)}, u32[]{:S(2)}) copy-start(s32[1,2,2]{2,1,0:T(2,128)} %hubs_ref.1) | copy-start | bytes 52

commit v2 on v1

v2 whole, which is shorter than its diff:
```python
import jax
import jax.numpy as jnp
from jax import lax
from jax.experimental import pallas as pl
from jax.experimental.pallas import tpu as pltpu
from jax.sharding import PartitionSpec as P

TILE = 512
TILES_DEV = 4
HUBS = 2
CAP = 32
N_ROW = 8
N_COL = 16
LANES = 128
CHUNK = 256
CHUNKS = TILES_DEV * TILE // CHUNK
FULL = 1 << 22
MESH = pl.DeviceIdType.MESH
F32 = jnp.float32
BF16 = jnp.bfloat16
NT = (((1,), (1,)), ((), ()))


def iota(shape, dim):
    return lax.broadcasted_iota(jnp.int32, shape, dim)


def one_hot(keys, rows):
    wide = jnp.broadcast_to(keys.astype(BF16), (rows, keys.shape[1]))
    return wide == iota((rows, keys.shape[1]), 0).astype(BF16)


def weighted(mask, values):
    return jnp.where(mask, jnp.broadcast_to(values.astype(BF16), mask.shape), jnp.zeros((), BF16))


def ones_where(mask):
    return jnp.where(mask, jnp.ones((), BF16), jnp.zeros((), BF16))


def two_rows(x, index):
    return jnp.concatenate([x[2 * index : 2 * index + 1], x[2 * index + 1 : 2 * index + 2]], axis=1)


def exchange_kernel(
    code_hbm, weight_hbm, count_hbm, degree_hbm, slots_ref, degrees_ref,
    code_ref, weight_ref, count_ref, wide, own_part, message, relay,
    in_sem, row_send, row_recv, col_send, col_recv, local_sem,
):
    row = lax.axis_index("row")
    col = lax.axis_index("col")
    row_peers = [lax.rem(row + k, N_ROW) for k in range(1, N_ROW)]
    col_peers = [lax.rem(col + k, N_COL) for k in range(1, N_COL)]

    barrier = pltpu.get_barrier_semaphore()
    for peer in col_peers:
        pl.semaphore_signal(barrier, inc=1, device_id=(row, peer), device_id_type=MESH)
    for peer in row_peers:
        pl.semaphore_signal(barrier, inc=1, device_id=(peer, col), device_id_type=MESH)
    mine = degrees_ref.at[col, row]
    inputs = [
        pltpu.make_async_copy(src, dst, in_sem.at[i])
        for i, (src, dst) in enumerate((
            (count_hbm, count_ref), (weight_hbm, weight_ref), (code_hbm, code_ref), (degree_hbm, mine),
        ))
    ]
    for copy in inputs:
        copy.start()
    for copy in inputs:
        copy.wait()

    lane = iota((32, LANES), 1)
    line = iota((32, LANES), 0)
    counts = jnp.where(lane // 4 == line, jnp.broadcast_to(count_ref[...], (32, LANES)), 0)
    spread = ones_where(iota((LANES, LANES), 0) % 4 == iota((LANES, LANES), 1) // CAP)
    counts = jnp.dot(counts.astype(BF16), spread, preferred_element_type=F32)
    for g in range(32):
        wide[pl.ds(g, 1), :] = weight_ref[:, pl.ds(g * LANES, LANES)].astype(F32)
    weights = jnp.where((lane % CAP).astype(F32) < counts, wide[...], 0.0)
    codes = code_ref[...]

    slab = jnp.where(weights > 0.0, (codes >> 15) - 32, -1)
    member = jnp.concatenate([ones_where(slab == j) for j in range(N_COL)], axis=0)
    upto = ones_where(jnp.logical_or(
        iota((LANES, 256), 0) <= iota((LANES, 256), 1), iota((LANES, 256), 1) >= LANES
    ))
    inside = jnp.dot(member, upto, preferred_element_type=F32)
    near = jnp.logical_and(
        iota((256, 256), 0) // 4 == iota((256, 256), 1) // 4, iota((256, 256), 1) < iota((256, 256), 0)
    )
    near = ones_where(near)
    rank = jnp.full((32, LANES), -1.0, F32)
    for half in range(2):
        part = inside[256 * half : 256 * half + 256]
        base = jnp.dot(near, part[:, LANES:].astype(BF16), preferred_element_type=F32)
        part = base + part[:, :LANES] - 1.0
        for j in range(8):
            rank = jnp.where(slab == 8 * half + j, part[32 * j : 32 * j + 32], rank)
    crowded = (jnp.max(rank, axis=(0, 1), keepdims=True) >= CAP).astype(F32) * FULL

    slab = slab.astype(F32)
    cell_low = (codes & 255).astype(F32)
    cell_high = ((codes >> 8) & 127).astype(F32)
    packed = []
    for r in range(N_ROW):
        part = jnp.zeros((N_COL, LANES), F32)
        for h in range(2):
            p = 2 * r + h
            mask = one_hot(two_rows(rank, p), CAP)
            none = jnp.zeros((CAP, 256), BF16)
            right = jnp.concatenate([
                weighted(mask, two_rows(cell_low, p)), none,
                weighted(mask, two_rows(cell_high, p)), weighted(mask, two_rows(weights, p)),
            ], axis=0)
            left = ones_where(one_hot(two_rows(slab, p), N_COL))
            part += lax.dot_general(left, right, NT, preferred_element_type=F32)
        packed.append(part)
    packed = jnp.concatenate(packed, axis=0)
    lanes = iota((LANES, LANES), 1)
    packed = jnp.where(lanes < 96, packed * 256.0 + pltpu.roll(packed, 64, axis=1), packed)

    flagged = codes.astype(F32) + crowded
    for u in range(4):
        left = pltpu.roll(flagged, (LANES - CAP * u) % LANES, axis=1)
        right = pltpu.roll(weights, (LANES + CAP - CAP * u) % LANES, axis=1)
        own_part[pl.ds(u, 32, stride=4), :] = jnp.where(lane < CAP, left, right)
    lines = jnp.where(lanes < 64, own_part[...], packed)
    for d in range(N_ROW * N_COL):
        message[d // N_COL, d % N_COL] = lines[d : d + 1]

    pl.semaphore_wait(barrier, N_ROW + N_COL - 2)

    def send(src, dst, send_sem, recv_sem, device):
        pltpu.make_async_remote_copy(
            src_ref=src, dst_ref=dst, send_sem=send_sem, recv_sem=recv_sem,
            device_id=device, device_id_type=MESH,
        ).start()

    for peer in row_peers:
        send(mine, mine, row_send.at[1], row_recv.at[1], (peer, col))
    for peer in row_peers:
        send(message.at[peer], relay.at[:, row], row_send.at[0], row_recv.at[0], (peer, col))
    own = pltpu.make_async_copy(message.at[row], relay.at[:, row], local_sem.at[0])
    own.start()
    own.wait()
    others = pl.ds(0, N_ROW - 1)
    rows_whole = (relay.at[:, others], degrees_ref.at[0, others])
    pltpu.make_async_copy(rows_whole[0], rows_whole[0], row_recv.at[0]).wait()
    for peer in col_peers:
        send(relay.at[peer], slots_ref.at[col], col_send.at[0], col_recv.at[0], (row, peer))
    own = pltpu.make_async_copy(relay.at[col], slots_ref.at[col], local_sem.at[1])
    own.start()
    pltpu.make_async_copy(rows_whole[1], rows_whole[1], row_recv.at[1]).wait()
    for peer in col_peers:
        send(degrees_ref.at[col], degrees_ref.at[col], col_send.at[1], col_recv.at[1], (row, peer))
    own.wait()
    others = pl.ds(0, N_COL - 1)
    cols_whole = (slots_ref.at[others], degrees_ref.at[others])
    for part in range(2):
        pltpu.make_async_copy(rows_whole[part], rows_whole[part], row_send.at[part]).wait()
    for part in range(2):
        pltpu.make_async_copy(cols_whole[part], cols_whole[part], col_send.at[part]).wait()
        pltpu.make_async_copy(cols_whole[part], cols_whole[part], col_recv.at[part]).wait()


def exchange(code, weight, count, degree):
    vmem = pl.BlockSpec(memory_space=pltpu.VMEM)
    hbm = pl.BlockSpec(memory_space=pltpu.HBM)
    pair = pltpu.SemaphoreType.DMA((2,))
    return pl.pallas_call(
        exchange_kernel,
        out_shape=(
            jax.ShapeDtypeStruct((N_COL, N_ROW, 1, LANES), F32),
            jax.ShapeDtypeStruct((N_COL, N_ROW, 4, LANES), F32),
        ),
        in_specs=[hbm] * 4,
        out_specs=(vmem, vmem),
        scratch_shapes=[
            pltpu.VMEM((32, LANES), jnp.int32),
            pltpu.VMEM((1, N_ROW * N_COL * CAP), BF16),
            pltpu.VMEM((1, LANES), jnp.int32),
            pltpu.VMEM((32, LANES), F32),
            pltpu.VMEM((LANES, LANES), F32),
            pltpu.VMEM((N_ROW, N_COL, 1, LANES), F32),
            pltpu.VMEM((N_COL, N_ROW, 1, LANES), F32),
            pltpu.SemaphoreType.DMA((4,)),
            pair, pair, pair, pair, pair,
        ],
        compiler_params=pltpu.CompilerParams(
            collective_id=0, has_side_effects=True, vmem_limit_bytes=16 << 20
        ),
    )(code, weight, count, degree)


def stored(block):
    return lax.rem(block, N_COL) * N_ROW + block // N_COL


def tile_kernel(
    slots_ref, degrees_ref, blocks_hbm, hubs_hbm, owned_ref, hub_ref, crowded_ref,
    blocks_ref, hubs_ref, hub_fields, fields, total, hub_total, staged, gathered, in_sem, out_sem,
):
    col = lax.axis_index("col")
    inputs = (
        pltpu.make_async_copy(blocks_hbm, blocks_ref, in_sem.at[0]),
        pltpu.make_async_copy(hubs_hbm, hubs_ref, in_sem.at[1]),
    )
    for copy in inputs:
        copy.start()

    turned = slots_ref[...].T
    code = turned[0:32].astype(jnp.int32)
    crowded_ref[0, 0] = (jnp.max(code) >= FULL).astype(jnp.int32)
    code = code & (FULL - 1)
    weight = turned[32:64]
    cell = turned[64:96].astype(jnp.int32)
    hub_weight = turned[96:128]
    hub_fields[0] = (((cell >> 8) & 1) * 64 + (cell >> 9)).astype(F32)
    hub_fields[1] = (cell & 255).astype(F32)
    hub_fields[2] = hub_weight
    used = jnp.max(jnp.where(hub_weight > 0.0, iota((32, LANES), 0) + 2, 0)) // 2

    chunk = jnp.where(weight > 0.0, code >> 17, CHUNKS)
    member = jnp.concatenate([ones_where(chunk == q) for q in range(CHUNKS)], axis=0)
    upto = ones_where(jnp.logical_or(
        iota((LANES, 256), 0) <= iota((LANES, 256), 1), iota((LANES, 256), 1) >= LANES
    ))
    inside = jnp.dot(member, upto, preferred_element_type=F32)
    inside, lines = inside[:, :LANES], inside[:, LANES:]
    before = ones_where(iota((256, 256), 1) < iota((256, 256), 0))
    base = jnp.dot(before, lines.astype(BF16), preferred_element_type=F32)
    rank = base + inside - 1.0
    place = jnp.full((32, LANES), -1.0, F32)
    for q in range(CHUNKS):
        place = jnp.where(chunk == q, rank[32 * q : 32 * q + 32], place)
    place = place.astype(jnp.int32)
    starts = [jnp.max(base[32 * q : 32 * q + 1]).astype(jnp.int32) for q in range(CHUNKS)]
    starts.append(jnp.max(base[255:256] + lines[255:256]).astype(jnp.int32))

    high, low = (place >> 7).astype(F32), (place & 127).astype(F32)
    parts = (
        (code & 255).astype(F32),
        (((code >> 8) & 1) + 2 * (code >> 17)).astype(F32),
        ((code >> 9) & 255).astype(F32),
        weight,
    )
    moved = jnp.zeros((LANES, LANES), F32)
    for p in range(16):
        mask = one_hot(two_rows(high, p), 32)
        left = jnp.concatenate([weighted(mask, two_rows(part, p)) for part in parts], axis=0)
        right = ones_where(one_hot(two_rows(low, p), LANES))
        moved += lax.dot_general(left, right, NT, preferred_element_type=F32)
    flags = moved[32:64].astype(jnp.int32)
    column = moved[0:32] + ((flags & 1) * 256).astype(F32)
    fields[0] = moved[64:96] + ((flags >> 1) * 256).astype(F32)
    fields[1] = column
    fields[2] = column - 256.0
    fields[3] = moved[96:128]

    scaling = jnp.sum(jnp.sum(degrees_ref[...], axis=0)) / (N_ROW * N_COL * TILE)
    for copy in inputs:
        copy.wait()
    gathered[...] = jnp.ones_like(gathered)
    for t in range(TILES_DEV):
        gathered[pl.ds(4 * t, 4), :] = degrees_ref[stored(blocks_ref[0, 0, t])]
    hub = col // 8
    hub_row = degrees_ref[stored(hubs_ref[0, hub, 0]), pl.ds(lax.rem(col, 8) // 2, 1), :]
    gathered[pl.ds(16, 8), :] = pltpu.roll(
        jnp.broadcast_to(hub_row, (8, LANES)), 64 * lax.rem(col, 2), axis=1
    )
    degree_rows = (scaling / gathered[...]).T

    def out_copy(q):
        return pltpu.make_async_copy(
            staged.at[q], owned_ref.at[q // 2, pl.ds(CHUNK * (q % 2), CHUNK)], out_sem.at[q]
        )

    for q in range(CHUNKS):
        total[...] = jnp.zeros_like(total)

        def add_block(b, _, q=q):
            def line(f):
                return jnp.concatenate(
                    [fields[f, pl.ds(2 * b, 1), :], fields[f, pl.ds(2 * b + 1, 1), :]], axis=1
                )

            left = weighted(one_hot(line(0) - 256.0 * q, CHUNK), line(3))
            right = jnp.concatenate(
                [ones_where(one_hot(line(1), 256)), ones_where(one_hot(line(2), 256))], axis=0
            )
            total[...] += lax.dot_general(left, right, NT, preferred_element_type=F32)
            return 0

        last = jnp.where(starts[q + 1] > starts[q], (starts[q + 1] + 255) >> 8, starts[q] >> 8)
        lax.fori_loop(starts[q] >> 8, last, add_block, 0)
        tile = q // 2
        degree = 1.0 / degrees_ref[stored(blocks_ref[0, 1, tile])]
        for j in range(2):
            rows = degree_rows[:, 4 * tile + 2 * (q % 2) + j][:, None]
            for n in range(4):
                values = total[pl.ds(LANES * j, LANES), pl.ds(LANES * n, LANES)]
                values = values * rows * degree[n : n + 1]
                staged[q, pl.ds(LANES * j, LANES), pl.ds(LANES * n, LANES)] = jnp.log(
                    jnp.maximum(values, 1.0)
                )
        out_copy(q).start()

    hub_total[...] = jnp.zeros_like(hub_total)

    def add_hub(b, _):
        def line(f):
            return jnp.concatenate(
                [hub_fields[f, pl.ds(2 * b, 1), :], hub_fields[f, pl.ds(2 * b + 1, 1), :]], axis=1
            )

        hub_total[...] += lax.dot_general(
            weighted(one_hot(line(0), LANES), line(2)), ones_where(one_hot(line(1), 256)),
            NT, preferred_element_type=F32,
        )
        return 0

    lax.fori_loop(0, used, add_hub, 0)
    hub_degree = 1.0 / degrees_ref[stored(hubs_ref[0, hub, 1])]
    for n in range(4):
        values = hub_total[pl.ds(64 * (n // 2), 64), pl.ds(LANES * (n % 2), LANES)]
        values = values * degree_rows[0:64, 16:17] * hub_degree[n : n + 1]
        hub_ref[:, pl.ds(LANES * n, LANES)] = jnp.log(jnp.maximum(values, 1.0))
    for q in range(CHUNKS):
        out_copy(q).wait()


def tiles(slots, degrees, blocks, hubs):
    vmem = pl.BlockSpec(memory_space=pltpu.VMEM)
    hbm = pl.BlockSpec(memory_space=pltpu.HBM)
    return pl.pallas_call(
        tile_kernel,
        out_shape=(
            jax.ShapeDtypeStruct((TILES_DEV, TILE, TILE), F32),
            jax.ShapeDtypeStruct((HUBS * TILE // N_COL, TILE), F32),
            jax.ShapeDtypeStruct((1, 1), jnp.int32),
        ),
        in_specs=[vmem, vmem, hbm, hbm],
        out_specs=(hbm, vmem, pl.BlockSpec(memory_space=pltpu.SMEM)),
        scratch_shapes=[
            pltpu.SMEM((1, 2, TILES_DEV), jnp.int32),
            pltpu.SMEM((1, HUBS, 2), jnp.int32),
            pltpu.VMEM((3, 32, LANES), F32),
            pltpu.VMEM((4, 32, LANES), F32),
            pltpu.VMEM((CHUNK, TILE), F32),
            pltpu.VMEM((LANES, 256), F32),
            pltpu.VMEM((CHUNKS, CHUNK, TILE), F32),
            pltpu.VMEM((LANES, LANES), F32),
            pltpu.SemaphoreType.DMA((2,)),
            pltpu.SemaphoreType.DMA((CHUNKS,)),
        ],
        compiler_params=pltpu.CompilerParams(vmem_limit_bytes=32 << 20),
    )(slots, degrees, blocks, hubs)


def dense_hub(code, weight, count, hubs, degrees):
    def to_owner(x):
        return lax.all_to_all(
            x.reshape(N_ROW * N_COL, -1), ("row", "col"), split_axis=0, concat_axis=0, tiled=True
        )

    codes, weights, counts = to_owner(code), to_owner(weight), to_owner(count)
    usable = jnp.arange(CAP, dtype=jnp.int32)[None, :] < counts
    weights = jnp.where(usable, weights, jnp.zeros((), BF16)).reshape(-1)
    codes = codes.reshape(-1) - TILES_DEV * TILE * TILE

    def step(turn, sums):
        part = lax.dynamic_slice_in_dim(codes, turn * 512, 512)
        value = lax.dynamic_slice_in_dim(weights, turn * 512, 512)
        left = jnp.where(
            (part >> 9)[:, None] == jnp.arange(HUBS * TILE, dtype=jnp.int32)[None, :],
            value[:, None], jnp.zeros((), BF16),
        )
        right = ((part & 511)[:, None] == jnp.arange(TILE, dtype=jnp.int32)[None, :]).astype(BF16)
        return sums + lax.dot_general(
            left, right, (((0,), (0,)), ((), ())), preferred_element_type=F32
        )

    sums = lax.fori_loop(
        0, codes.shape[0] // 512, step, jnp.zeros((HUBS * TILE, TILE), F32)
    )
    sums = sums.reshape(N_COL, HUBS * TILE // N_COL, TILE)
    sums = jnp.sum(lax.all_to_all(sums, "col", 0, 0, tiled=True), axis=0)
    slab_rows = HUBS * TILE // N_COL
    offset = lax.axis_index("col") * slab_rows
    degrees = degrees.reshape(N_ROW * N_COL, TILE)
    scaling = jnp.mean(degrees)
    pair = lax.dynamic_index_in_dim(hubs[0], offset // TILE, 0, keepdims=False)
    row_degree = lax.dynamic_index_in_dim(degrees, stored(pair[0]), 0, keepdims=False)
    row_degree = lax.dynamic_slice_in_dim(row_degree, lax.rem(offset, TILE), slab_rows)
    col_degree = lax.dynamic_index_in_dim(degrees, stored(pair[1]), 0, keepdims=False)
    return jnp.log(
        jnp.maximum(scaling * sums / (row_degree[:, None] * col_degree[None, :]), 1.0)
    )


def shards(edge_code, edge_weight, edge_count, tile_blocks, hub_blocks, node_degree):
    slots, degrees = exchange(
        edge_code.reshape(32, LANES), edge_weight, edge_count, node_degree.reshape(4, LANES)
    )
    degrees = degrees.reshape(N_COL * N_ROW, 4, LANES)
    owned, hub, crowded = tiles(
        slots.reshape(-1, LANES), degrees, tile_blocks.transpose(0, 2, 1), hub_blocks
    )
    hub = lax.cond(
        crowded[0, 0] > 0,
        lambda: dense_hub(edge_code, edge_weight, edge_count, hub_blocks, degrees),
        lambda: hub,
    )
    return owned, hub


def solution(mesh):
    both = ("row", "col")
    return jax.shard_map(
        shards,
        mesh=mesh,
        in_specs=(
            P(both, None), P(both, None), P(both, None),
            P(both, None, None), P("row", None, None), P(both, None),
        ),
        out_specs=(P(both, None, None), P(both, None)),
        check_vma=False,
    )
```

time: 39.1 us -> 28.9 us (0.74)
  the two profiles are of different devices: /device:TPU:24 before, /device:TPU:0 now
where the time goes in v2:
time: 28.9 us; the launch traced here: 28.6 us
  Pallas kernels  25.3 us (88%)
  local copies, waits for them, and re-layouts  2 us (7%)
  between operations  1.33 us (5%)
    pallas_call x1, Pallas kernels, exchange(): pl.pallas_call(exchange_kernel, out_shape=(jax.ShapeDtypeStruct((N_COL, N...  17.8 us
    pallas_call x1, Pallas kernels, tiles(): pl.pallas_call(tile_kernel, out_shape=(jax.ShapeDtypeStruct((TILES_DEV, T...  7.49 us
    unnamed x6, local copies, waits for them, and re-layouts  2 us

profile of v2, /device:TPU:0, one launch (start us, length us, event | category | flops | bytes accessed | tf_op | source)
XLA Modules:
  0.0 28.6 jit_solution(2252570325813718691)
XLA Ops:
  0.6 0.0 copy-start
  0.6 0.7 %copy-done = f32[1,512]{1,0:T(1,128)S(1)} copy-done((f32[1,512]{1,0:T(1,128)S(1)}, f32[1,512]{1,0:T(1,128)}, u32[]{:S(2)}) %copy-start) | copy-done | bytes 2072
  1.3 17.8 %shard_map.77 = (f32[16,8,1,128]{3,2,1,0:T(1,128)S(1)}, f32[16,8,4,128]{3,2,1,0:T(4,128)S(1)}) custom-call(s32[32,128]{1,0:T(8,128)} %bitcast.24, bf16[1,4096]{1,0:T(2,128)(2,1)} %weight_hbm.1, s32[1,128]{1,0:T(1,128)} %count_hbm.1, f32[4,128]{1,0:T(4,128)S(1)} %bitcast.18), custom_call_target="tpu_custom_call" | custom-call | tf_op jit(solution)/shard_map/pallas_call | solution.py:170
  19.1 0.0 copy-start.1
  19.1 0.7 %copy-done.1 = s32[1,4,2]{1,2,0:T(2,128)S(1)} copy-done((s32[1,4,2]{1,2,0:T(2,128)S(1)}, s32[1,4,2]{1,2,0:T(2,128)}, u32[]{:S(2)}) %copy-start.1) | copy-done | bytes 56
  19.8 7.5 %shard_map.78 = (f32[4,512,512]{2,1,0:T(8,128)}, f32[64,512]{1,0:T(8,128)S(1)}, s32[1,1]{1,0:T(1,128)}) custom-call(f32[128,128]{1,0:T(8,128)S(1)} %bitcast.17, f32[128,4,128]{2,1,0:T(4,128)S(1)} %bitcast.20, s32[1,2,4]{2,1,0:T(2,128)S(1)} %bitcast.19, s32[1,2,2]{2,1,0:T(2,128)} %hubs_hbm.1), custom_call_target="tpu_custom_call" | custom-call | tf_op jit(solution)/shard_map/pallas_call | solution.py:335
  28.0 0.0 copy-start.4
  28.0 0.6 %copy-done.4 = f32[64,512]{1,0:T(8,128)} copy-done((f32[64,512]{1,0:T(8,128)}, f32[64,512]{1,0:T(8,128)S(1)}, u32[]{:S(2)}) %copy-start.4) | copy-done | bytes 131096
  (1 shorter events, 0.0 us)
Async XLA Ops:
  0.6 0.7 %copy-start = (f32[1,512]{1,0:T(1,128)S(1)}, f32[1,512]{1,0:T(1,128)}, u32[]{:S(2)}) copy-start(f32[1,512]{1,0:T(1,128)} %param.15) | copy-start | bytes 6148
  19.1 0.7 %copy-start.1 = (s32[1,4,2]{1,2,0:T(2,128)S(1)}, s32[1,4,2]{1,2,0:T(2,128)}, u32[]{:S(2)}) copy-start(s32[1,4,2]{1,2,0:T(2,128)} %param.13) | copy-start | bytes 100
  28.0 0.7 %copy-start.4 = (f32[64,512]{1,0:T(8,128)}, f32[64,512]{1,0:T(8,128)S(1)}, u32[]{:S(2)}) copy-start(f32[64,512]{1,0:T(8,128)S(1)} %get-tuple-element.210) | copy-start | bytes 393220
